TPU v7x, 1024 devices: a whole 4x4x32 slice. The times are simulated.
1024 devices in a mesh: tensor: 32 (over z_hi, y, core), context: 32 (over z_lo, x).
Axes of the slice: x: 4, y: 4, z: 32 (z_hi: 4, z_lo: 8; z = z_hi * 8 + z_lo), core: 2. Of those that a mesh axis runs over, the one named last changes fastest.
Arguments:
- query_rows: bfloat16 [8192, 8192], P('context', 'tensor'), may hold values from -160 to 160, as said below
- key_rows: bfloat16 [8192, 1024], P('context'), may hold values from -5 to 5, as said below
- value_rows: bfloat16 [8192, 1024], P('context'), may hold values from -6 to 6
- doc_ids: int32 [8192], P('context'), may hold values from 0 to 15, never falling along the last dimension, each value on 1 to 1024 neighbouring positions
- out_weight: bfloat16 [8192, 8192], P('tensor'), may hold values from -0.125 to 0.125
Outputs:
- mixed: bfloat16 [8192, 8192], P('context', 'tensor')
Inputs may be any that keep to these rules, and one draw needn't show every extreme that they name: `query_rows`: within the range given by the table of arrays. `key_rows`: within the range given by the table of arrays. `doc_ids`: document numbers never fall along the sequence; every document has 1 to 1024 tokens and one has exactly 1024.
All inputs are finite; a program needn't handle non-finite values.
Results may differ from a plain program's by a relative error of at most 0.015.
Values may be sent and summed in bfloat16 or wider, within the bound.
A program may use at most 64 MiB of HBM per device.

v0:
```python
import jax
import jax.numpy as jnp
from jax import lax
from jax.sharding import PartitionSpec as P

H = 64
KVH = 8
HD = 128


NEG_BIG = -1e30


def in_one_piece(arrays, axis, dim, along):
    both = jnp.concatenate(arrays, axis=along)
    result, at, gathered = (lax.all_gather(both, axis, axis=dim, tiled=True), 0, [])
    for a in arrays:
        gathered.append(lax.slice_in_dim(result, at, at + a.shape[along], axis=along))
        at += a.shape[along]
    return tuple(gathered)


def absorb(running, grouped, query_pos, query_docs, key_block, value_block, doc_block):
    running_max, running_sum, numer = running
    kv_count = grouped.shape[1]
    key_heads = key_block.reshape(key_block.shape[0], kv_count, HD)
    value_heads = value_block.reshape(value_block.shape[0], kv_count, HD)
    key_pos = jnp.arange(key_block.shape[0], dtype=jnp.int32)
    allowed = (
        (key_pos[None, :] <= query_pos[:, None])
        & (doc_block[None, :] == query_docs[:, None])
        & True
    )
    scores = jnp.einsum(
        "tkgd,skd->kgts", grouped, key_heads, preferred_element_type=jnp.float32
    ) * HD ** (-0.5)
    scores = jnp.where(allowed, scores, NEG_BIG)
    fresh_max = jnp.maximum(running_max, jnp.max(scores, axis=-1))
    weights = jnp.where(allowed, jnp.exp(scores - fresh_max[..., None]), 0.0)
    running_sum = jnp.sum(weights, axis=-1)
    numer = jnp.einsum(
        "kgts,skd->kgtd",
        weights.astype(jnp.bfloat16),
        value_heads,
        preferred_element_type=jnp.float32,
    )
    return (fresh_max, running_sum, numer)


def body(query_rows, key_rows, value_rows, doc_ids, out_weight):
    tokens_here = query_rows.shape[0]
    local_heads = query_rows.shape[1] // HD
    group_size = H // KVH
    kv_count = max(1, local_heads // group_size)
    per_kv = local_heads // kv_count
    first_kv = lax.axis_index("tensor") * local_heads // group_size
    key_local = lax.dynamic_slice_in_dim(key_rows, first_kv * HD, kv_count * HD, 1)
    value_local = lax.dynamic_slice_in_dim(value_rows, first_kv * HD, kv_count * HD, 1)
    grouped = query_rows.reshape(tokens_here, kv_count, per_kv, HD)
    block_index = lax.axis_index("context")
    query_pos = block_index * tokens_here + jnp.arange(tokens_here, dtype=jnp.int32)
    initial = (
        jnp.full((kv_count, per_kv, tokens_here), NEG_BIG, jnp.float32),
        jnp.zeros((kv_count, per_kv, tokens_here), jnp.float32),
        jnp.zeros((kv_count, per_kv, tokens_here, HD), jnp.float32),
    )
    pieces = (
        *in_one_piece((key_local, value_local), "context", 0, 1),
        lax.all_gather(doc_ids, "context", axis=0, tiled=True),
    )
    running = absorb(initial, grouped, query_pos, doc_ids, pieces[0], pieces[1], pieces[2])
    final_max, final_sum, numer = running
    attended = numer / final_sum[..., None]
    attended = (
        attended.transpose(2, 0, 1, 3).reshape(tokens_here, local_heads * HD).astype(jnp.bfloat16)
    )
    summed = lax.psum_scatter(
        lax.dot_general(
            out_weight, attended, (((0,), (1,)), ((), ())), preferred_element_type=jnp.float32
        ).astype(jnp.bfloat16),
        "tensor",
        scatter_dimension=0,
        tiled=True,
    ).astype(jnp.float32)
    return summed.T.astype(jnp.bfloat16)


def solution(mesh):
    placed = (
        P("context", "tensor"),
        P("context", None),
        P("context", None),
        P("context"),
        P("tensor", None),
    )
    return jax.shard_map(
        body, mesh=mesh, in_specs=placed, out_specs=P("context", "tensor"), check_vma=False
    )
```

profile of v0, /device:TPU:2, one launch (start us, length us, event | category | flops | bytes accessed | tf_op | source)
XLA Modules:
  0.0 507.9 jit_solution(6065523191434086240)
XLA Ops:
  6.5 0.0 copy-start
  6.5 0.0 all-gather.3.cloned.1.call-start
  6.5 0.9 constant_dynamic-slice_fusion
  7.5 0.7 pad_maximum_fusion
  8.1 0.0 all-gather.3.cloned.1.call-update
  8.2 0.0 reduce-scatter.2.cloned.1.call-start
  8.2 124.7 %all-gather = s32[32,1,256]{2,1,0:T(1,128)S(1)} all-gather(s32[1,1,256]{2,1,0:T(1,128)} %bitcast.61), channel_id=1, replica_groups=mesh['tensor'=32,'context'=32] {'context'}, dimensions={0}, use_global_device_ids=true | all-gather | bytes 33792 | tf_op jit(solution)/shard_map/all_gather | solution.py:69
  132.9 4.4 fusion.7
  137.4 117.5 %all-gather.3.cloned.1.call-done = bf16[8192,256]{1,0:T(8,128)(2,1)} async-done(((bf16[256,256]{1,0:T(8,128)(2,1)}), bf16[8192,256]{1,0:T(8,128)(2,1)}) %all-gather.3.cloned.1.call-update) | async-done | bytes 4194320 | tf_op jit(solution)/shard_map/all_gather | solution.py:16
  254.9 0.0 copy-done
  254.9 4.5 fusion
  259.3 4.5 fusion.1
  263.8 5.7 %fusion.13 = bf16[2,256,128]{1,2,0:T(8,128)(2,1)S(1)} fusion(bf16[8192,256]{1,0:T(8,128)(2,1)} %all-gather.3.cloned.1.call-done, f32[8192,256,2]{1,0,2:T(8,128)S(1)} %get-tuple-element.6, f32[2,256]{1,0:T(2,128)S(1)} %broadcast_maximum_fusion, pred[256,8192]{0,1:T(8,128)(4,1)S(1)} %fusion.7, f32[2,256]{1,0:T(2,128)S(1)} %fusion.1), kind=kOutput, calls=%fused_computation.16 | convolution fusion | flops 1094844416 | bytes 21106688 | tf_op jit(solution)/shard_map/kgts,skd->kgtd/dot_general | solution.py:41
  269.5 5.4 %fusion.3 = bf16[8192,256]{0,1:T(8,128)(2,1)} fusion(bf16[256,256]{0,1:T(8,128)(2,1)S(1)} %bitcast.59, bf16[256,8192]{1,0:T(8,128)(2,1)} %param.9), kind=kOutput, calls=%fused_computation.6 | convolution fusion | flops 1075838976 | bytes 8519680 | tf_op jit(solution)/shard_map/dot_general | solution.py:78
  274.9 0.0 reduce-scatter.2.cloned.1.call-update
  274.9 226.2 %reduce-scatter.2.cloned.1.call-done = bf16[256,256]{0,1:T(8,128)(2,1)} async-done(((bf16[8192,256]{0,1:T(8,128)(2,1)}), bf16[256,256]{0,1:T(8,128)(2,1)}) %reduce-scatter.2.cloned.1.call-update) | async-done | bytes 131088 | tf_op jit(solution)/shard_map/reduce_scatter | solution.py:77
  (2 shorter events, 0.0 us)
Async XLA Ops:
  6.5 248.3 %copy-start = (bf16[256,256]{1,0:T(8,128)(2,1)S(1)}, bf16[256,256]{1,0:T(8,128)(2,1)}, u32[]{:S(2)}) copy-start(bf16[256,256]{1,0:T(8,128)(2,1)} %param.5) | copy-start | bytes 393220
  6.5 248.3 %all-gather.3.cloned.1.call-start = ((), (), s32[]{:S(2)}) async-start(), calls=%async_computation.1 | async-start | bytes 4325376 | tf_op jit(solution)/shard_map/all_gather | solution.py:16
  8.2 492.9 %reduce-scatter.2.cloned.1.call-start = ((), (), s32[]{:S(2)}) async-start(), calls=%async_computation.2 | async-start | bytes 4325376 | tf_op jit(solution)/shard_map/reduce_scatter | solution.py:77
Sparse Core Ops, SparseCore 0:
  10.0 244.8 all-gather.2
  275.0 226.0 reduce-scatter.1
where the time goes:
time: 508 us
  waiting for transfers between devices  344 us (68%)
  blocking collectives  125 us (25%)
  matrix products  15.5 us (3%)
  between operations  13.4 us (3%)
  other arithmetic  9.56 us (2%)
    reduce_scatter x1, waiting for transfers between devices, body(): lax.psum_scatter(lax.dot_general(out_weight, attended, (((0,), (1,)), (()...  226 us
    all_gather x1, blocking collectives, body(): lax.all_gather(doc_ids, 'context', axis=0, tiled=True)  125 us
    all_gather x1, waiting for transfers between devices, in_one_piece(): lax.all_gather(both, axis, axis=dim, tiled=True)  117 us
  transfers between devices with their start and end apart: 2, of which 2 were waited for; matrix products, arithmetic and copies ran while one was open for 1% of the time, Pallas kernels for 0%

commit v1 on v0

v1 whole, which is shorter than its diff:
```python
import jax
import jax.numpy as jnp
from jax import lax
from jax.experimental import pallas as pl
from jax.experimental.pallas import tpu as pltpu
from jax.sharding import PartitionSpec as P

HD = 128
GROUP = 8
BACK = 4
TOK = 256
HALF = TOK // 2
NEG_BIG = -1e30
SCALE = HD**-0.5 * 1.4426950408889634
MESH = pl.DeviceIdType.MESH
OFFSETS = (2, 1, 3, 0)
BLOCKS = BACK + 1
KEYS = BLOCKS * TOK


def kernel(
    n_ctx,
    q_ref,
    k_ref,
    v_ref,
    doc_ref,
    w_ref,
    out_ref,
    kv,
    docs,
    dq,
    s_buf,
    m_buf,
    p_buf,
    l_buf,
    a_buf,
    w_buf,
    p_out,
    y_in,
    z_out,
    z_in,
    loc_sem,
    w_sem,
    wx_send,
    wx_recv,
    kv_send,
    kv_recv,
    doc_send,
    doc_recv,
    fwd_send,
    fwd_recv,
    a_send,
    a_recv,
    y_send,
    y_recv,
    z_send,
    z_recv,
):
    c = lax.axis_index("context")
    t = lax.axis_index("tensor")
    core = lax.rem(t, 2)
    y = lax.rem(t // 2, 4)
    z = t // 8
    other = 1 - core

    def dev(dz, dy, same_core=True):
        who = core if same_core else other
        return {"tensor": (lax.rem(z + dz, 4) * 4 + lax.rem(y + dy, 4)) * 2 + who}

    barrier = pltpu.get_barrier_semaphore()
    for where in (dev(0, 0, False), dev(0, 1), dev(0, 3), dev(1, 0), dev(3, 0)):
        pl.semaphore_signal(barrier, inc=1, device_id=where, device_id_type=MESH)
    for k in range(1, BACK + 1):

        @pl.when(c + k < n_ctx)
        def _():
            pl.semaphore_signal(
                barrier, inc=1, device_id={"context": c + k}, device_id_type=MESH
            )

        @pl.when(c >= k)
        def _():
            pl.semaphore_signal(
                barrier, inc=1, device_id={"context": c - k}, device_id_type=MESH
            )

    head = pl.multiple_of((t // 4) * HD, HD)
    k_copy = pltpu.make_async_copy(
        k_ref.at[:, pl.ds(head, HD)], kv.at[0, pl.ds(0, TOK), :], loc_sem.at[0]
    )
    v_copy = pltpu.make_async_copy(
        v_ref.at[:, pl.ds(head, HD)], kv.at[1, pl.ds(0, TOK), :], loc_sem.at[1]
    )
    k_copy.start()
    v_copy.start()

    def columns(r, q, who):
        j = lax.rem(z + OFFSETS[r], 4) * 4 + lax.rem(y + OFFSETS[q], 4)
        return pl.ds(pl.multiple_of((j * 2 + who) * TOK, TOK), TOK)

    def w_local(r, q):
        i = r * 4 + q
        return pltpu.make_async_copy(
            w_ref.at[:, columns(r, q, core)], w_buf.at[i, core], w_sem.at[i]
        )

    def w_cross(r, q):
        i = r * 4 + q
        return pltpu.make_async_remote_copy(
            src_ref=w_ref.at[:, columns(r, q, other)],
            dst_ref=w_buf.at[i, core],
            send_sem=wx_send.at[i],
            recv_sem=wx_recv.at[i],
            device_id=dev(0, 0, False),
            device_id_type=MESH,
        )

    def w_cross_in(r, q):
        i = r * 4 + q
        return pltpu.make_async_remote_copy(
            src_ref=w_ref.at[:, columns(r, q, other)],
            dst_ref=w_buf.at[i, other],
            send_sem=wx_send.at[i],
            recv_sem=wx_recv.at[i],
            device_id=dev(0, 0, False),
            device_id_type=MESH,
        )

    for r in range(4):
        for q in range(4):
            w_local(r, q).start()

    row = doc_ref[...]
    docs[0] = jnp.broadcast_to(row, (8, TOK))
    dq[...] = jnp.broadcast_to(row, (TOK, TOK)).T
    for k in range(1, BACK + 1):

        @pl.when(c < k)
        def _():
            kv[:, pl.ds(k * TOK, TOK), :] = jnp.zeros((2, TOK, HD), jnp.bfloat16)
            docs[k] = jnp.full((8, TOK), -1, jnp.int32)

    k_copy.wait()
    v_copy.wait()
    partners = 5 + jnp.minimum(c, BACK) + jnp.minimum(n_ctx - 1 - c, BACK)
    pl.semaphore_wait(barrier, partners)

    def kv_out(k):
        return pltpu.make_async_remote_copy(
            src_ref=kv.at[core, pl.ds(0, TOK), :],
            dst_ref=kv.at[core, pl.ds(k * TOK, TOK), :],
            send_sem=kv_send.at[k - 1],
            recv_sem=kv_recv.at[k - 1],
            device_id={"context": c + k},
            device_id_type=MESH,
        )

    def doc_out(k):
        return pltpu.make_async_remote_copy(
            src_ref=docs.at[0],
            dst_ref=docs.at[k],
            send_sem=doc_send.at[k - 1],
            recv_sem=doc_recv.at[k - 1],
            device_id={"context": c + k},
            device_id_type=MESH,
        )

    def forward(k, who):
        return pltpu.make_async_remote_copy(
            src_ref=kv.at[who, pl.ds(k * TOK, TOK), :],
            dst_ref=kv.at[who, pl.ds(k * TOK, TOK), :],
            send_sem=fwd_send.at[k - 1],
            recv_sem=fwd_recv.at[k - 1],
            device_id=dev(0, 0, False),
            device_id_type=MESH,
        )

    for k in range(1, BACK + 1):

        @pl.when(c + k < n_ctx)
        def _():
            doc_out(k).start()
            kv_out(k).start()

    for r in range(4):
        for q in range(4):
            w_cross(r, q).start()

    def scores(k):
        keys = kv[0, pl.ds(k * TOK, TOK), :]
        mask = dq[...] == docs[k, 0:1, :]
        if k == 0:
            i = lax.broadcasted_iota(jnp.int32, (TOK, TOK), 0)
            j = lax.broadcasted_iota(jnp.int32, (TOK, TOK), 1)
            mask = mask & (j <= i)
        for h in range(2):
            s = lax.dot_general(
                q_ref[:, pl.ds(h * HD, HD)],
                keys,
                (((1,), (1,)), ((), ())),
                preferred_element_type=jnp.float32,
            )
            s = jnp.where(mask, s * SCALE, NEG_BIG)
            rows = pl.ds(h * TOK, TOK)
            s_buf[k, rows, :] = s
            if k == 0:
                m_buf[rows, :] = s
            else:
                m_buf[rows, :] = jnp.maximum(m_buf[rows, :], s)

    scores(0)
    for k in range(1, BACK + 1):

        @pl.when(c >= k)
        def _():
            kv_out(k).wait_recv()
            forward(k, core).start()

        if k >= 2:

            @pl.when(c >= k - 1)
            def _():
                forward(k - 1, other).wait_recv()
                doc_out(k - 1).wait_recv()

            scores(k - 1)

    @pl.when(c >= BACK)
    def _():
        forward(BACK, other).wait_recv()
        doc_out(BACK).wait_recv()

    scores(BACK)

    def softmax(i, carry):
        rows = pl.ds(pl.multiple_of(i * 64, 64), 64)
        top = jnp.max(m_buf[rows, :], axis=-1, keepdims=True)
        total = jnp.zeros((64, TOK), jnp.float32)
        for k in range(BLOCKS):
            e = jnp.exp2(s_buf[k, rows, :] - top)
            total = total + e
            p_buf[rows, pl.ds(k * TOK, TOK)] = e.astype(jnp.bfloat16)
        l_buf[rows, :] = jnp.broadcast_to(jnp.sum(total, axis=-1, keepdims=True), (64, HD))
        return carry

    lax.fori_loop(0, 8, softmax, 0)
    for h in range(2):
        rows = pl.ds(h * TOK, TOK)
        o = jnp.dot(p_buf[rows, :], kv[1], preferred_element_type=jnp.float32)
        a_buf[core, :, pl.ds(h * HD, HD)] = (o / l_buf[rows, :]).astype(jnp.bfloat16)

    def a_copy(who):
        return pltpu.make_async_remote_copy(
            src_ref=a_buf.at[who],
            dst_ref=a_buf.at[who],
            send_sem=a_send.at[0],
            recv_sem=a_recv.at[0],
            device_id=dev(0, 0, False),
            device_id_type=MESH,
        )

    a_copy(core).start()
    for r in range(4):
        for q in range(4):
            w_local(r, q).wait()
            w_cross_in(r, q).wait_recv()
    a_copy(other).wait_recv()

    lo, hi = pl.ds(0, HALF), pl.ds(HALF, HALF)

    def project(r, q):
        i = r * 4 + q
        p = jnp.dot(a_buf[0], w_buf[i, 0], preferred_element_type=jnp.float32)
        p = p + jnp.dot(a_buf[1], w_buf[i, 1], preferred_element_type=jnp.float32)
        p_out[r, q] = p.astype(jnp.bfloat16)

    def y_copy(r, slot, src):
        return pltpu.make_async_remote_copy(
            src_ref=src,
            dst_ref=y_in.at[r, slot],
            send_sem=y_send.at[r, slot],
            recv_sem=y_recv.at[r, slot],
            device_id=dev(0, 1 if slot % 2 == 0 else 3),
            device_id_type=MESH,
        )

    def y_src(r, slot):
        q, half = ((0, lo), (0, hi), (1, hi), (2, lo), (1, lo), (2, hi))[slot]
        return p_out.at[r, q, half, :]

    def y_start(r, slot):
        y_copy(r, slot, y_src(r, slot)).start()

    def y_got(r, slot):
        y_copy(r, slot, y_src(r, slot)).wait_recv()
        return y_in[r, slot].astype(jnp.float32)

    def stage_a(r):
        project(r, 0)
        y_start(r, 0)
        y_start(r, 1)

    def stage_d(r):
        project(r, 1)
        y_start(r, 2)
        project(r, 2)
        y_start(r, 3)
        project(r, 3)

    def stage_b(r):
        up = p_out[r, 1, lo, :].astype(jnp.float32) + y_got(r, 0)
        p_out[r, 1, lo, :] = up.astype(jnp.bfloat16)
        y_start(r, 4)
        down = p_out[r, 2, hi, :].astype(jnp.float32) + y_got(r, 1)
        p_out[r, 2, hi, :] = down.astype(jnp.bfloat16)
        y_start(r, 5)

    def y_sum(r):
        low = p_out[r, 3, lo, :].astype(jnp.float32) + y_got(r, 3) + y_got(r, 4)
        high = p_out[r, 3, hi, :].astype(jnp.float32) + y_got(r, 2) + y_got(r, 5)
        return low, high

    def z_copy(slot):
        r, half = ((0, lo), (0, hi), (1, hi), (2, lo), (1, lo), (2, hi))[slot]
        return pltpu.make_async_remote_copy(
            src_ref=z_out.at[r, half, :],
            dst_ref=z_in.at[slot],
            send_sem=z_send.at[slot],
            recv_sem=z_recv.at[slot],
            device_id=dev(1 if slot % 2 == 0 else 3, 0),
            device_id_type=MESH,
        )

    def z_got(slot):
        z_copy(slot).wait_recv()
        return z_in[slot].astype(jnp.float32)

    def y_done(r):
        low, high = y_sum(r)
        z_out[r, lo, :] = low.astype(jnp.bfloat16)
        z_out[r, hi, :] = high.astype(jnp.bfloat16)
        if r == 0:
            z_copy(0).start()
            z_copy(1).start()
        elif r == 1:
            z_copy(2).start()
        else:
            z_copy(3).start()

    stage_a(0)
    stage_d(0)
    stage_a(1)
    stage_b(0)
    stage_d(1)
    stage_a(2)
    stage_b(1)
    stage_d(2)
    stage_a(3)
    y_done(0)
    stage_b(2)
    stage_d(3)
    y_done(1)
    stage_b(3)
    y_done(2)
    own_low, own_high = y_sum(3)
    up = z_out[1, lo, :].astype(jnp.float32) + z_got(0)
    z_out[1, lo, :] = up.astype(jnp.bfloat16)
    z_copy(4).start()
    down = z_out[2, hi, :].astype(jnp.float32) + z_got(1)
    z_out[2, hi, :] = down.astype(jnp.bfloat16)
    z_copy(5).start()
    own_low = own_low + z_got(3)
    own_high = own_high + z_got(2)
    out_ref[lo, :] = (own_low + z_got(4)).astype(jnp.bfloat16)
    out_ref[hi, :] = (own_high + z_got(5)).astype(jnp.bfloat16)

    for k in range(1, BACK + 1):

        @pl.when(c + k < n_ctx)
        def _():
            doc_out(k).wait_send()
            kv_out(k).wait_send()

        @pl.when(c >= k)
        def _():
            forward(k, core).wait_send()

    a_copy(core).wait_send()
    for r in range(4):
        for q in range(4):
            w_cross(r, q).wait_send()
        for slot in range(6):
            y_copy(r, slot, y_src(r, slot)).wait_send()
    for slot in range(6):
        z_copy(slot).wait_send()


def solution(mesh):
    n_ctx = mesh.shape["context"]

    def body(query_rows, key_rows, value_rows, doc_ids, out_weight):
        dma = pltpu.SemaphoreType.DMA
        bf16, f32 = jnp.bfloat16, jnp.float32
        vmem = pl.BlockSpec(memory_space=pltpu.VMEM)
        hbm = pl.BlockSpec(memory_space=pltpu.HBM)

        def run(*refs):
            kernel(n_ctx, *refs)

        return pl.pallas_call(
            run,
            out_shape=jax.ShapeDtypeStruct((TOK, TOK), bf16),
            in_specs=[vmem, hbm, hbm, vmem, hbm],
            out_specs=vmem,
            scratch_shapes=[
                pltpu.VMEM((2, KEYS, HD), bf16),
                pltpu.VMEM((BLOCKS, 8, TOK), jnp.int32),
                pltpu.VMEM((TOK, TOK), jnp.int32),
                pltpu.VMEM((BLOCKS, 2 * TOK, TOK), f32),
                pltpu.VMEM((2 * TOK, TOK), f32),
                pltpu.VMEM((2 * TOK, KEYS), bf16),
                pltpu.VMEM((2 * TOK, HD), f32),
                pltpu.VMEM((2, TOK, TOK), bf16),
                pltpu.VMEM((16, 2, TOK, TOK), bf16),
                pltpu.VMEM((4, 4, TOK, TOK), bf16),
                pltpu.VMEM((4, 6, HALF, TOK), bf16),
                pltpu.VMEM((3, TOK, TOK), bf16),
                pltpu.VMEM((6, HALF, TOK), bf16),
                dma((2,)),
                dma((16,)),
                dma((16,)),
                dma((16,)),
                dma((BACK,)),
                dma((BACK,)),
                dma((BACK,)),
                dma((BACK,)),
                dma((BACK,)),
                dma((BACK,)),
                dma((1,)),
                dma((1,)),
                dma((4, 6)),
                dma((4, 6)),
                dma((6,)),
                dma((6,)),
            ],
            compiler_params=pltpu.CompilerParams(
                collective_id=0, has_side_effects=True, vmem_limit_bytes=60 * 2**20
            ),
        )(query_rows, key_rows, value_rows, doc_ids.reshape(1, TOK), out_weight)

    placed = (
        P("context", "tensor"),
        P("context", None),
        P("context", None),
        P("context"),
        P("tensor", None),
    )
    return jax.shard_map(
        body, mesh=mesh, in_specs=placed, out_specs=P("context", "tensor"), check_vma=False
    )
```

time: 508 us -> 88.4 us (0.17)
  the two profiles are of different devices: /device:TPU:2 before, /device:TPU:4 now
where the time goes in v1:
time: 88.4 us; the launch traced here: 88 us
  Pallas kernels  86.5 us (98%)
  local copies, waits for them, and re-layouts  1.57 us (2%)
    pallas_call x1, Pallas kernels, body(): pl.pallas_call(run, out_shape=jax.ShapeDtypeStruct((TOK, TOK), bf16), in_...  86.5 us

profile of v1, /device:TPU:4, one launch (start us, length us, event | category | flops | bytes accessed | tf_op | source)
XLA Modules:
  0.0 88.0 jit_solution(6670185706293995849)
XLA Ops:
  0.0 86.5 %shard_map.55 = bf16[256,256]{1,0:T(8,128)(2,1)} custom-call(bf16[256,256]{1,0:T(8,128)(2,1)} %refs_0_.1, bf16[256,1024]{1,0:T(8,128)(2,1)} %refs_1_.1, bf16[256,1024]{1,0:T(8,128)(2,1)} %refs_2_.1, s32[1,256]{1,0:T(1,128)} %bitcast.1, bf16[256,8192]{1,0:T(8,128)(2,1)} %refs_4_.1), custom_call_target="tpu_custom_call" | custom-call | tf_op jit(solution)/shard_map/pallas_call | solution.py:410
  86.5 1.6 %copy.7 = bf16[256,256]{1,0:T(8,128)(2,1)} copy(bf16[256,256]{1,0:T(8,128)(2,1)} %shard_map.55) | data formatting | bytes 262144

commit v2 on v1

v2 whole, which is shorter than its diff:
```python
import jax
import jax.numpy as jnp
from jax import lax
from jax.experimental import pallas as pl
from jax.experimental.pallas import tpu as pltpu
from jax.sharding import PartitionSpec as P

HD = 128
GROUP = 8
BACK = 4
TOK = 256
HALF = TOK // 2
NEG_BIG = -1e30
SCALE = HD**-0.5 * 1.4426950408889634
MESH = pl.DeviceIdType.MESH
OFFSETS = (2, 1, 3, 0)
ORDER = ((1, 2, 3, 0), (0, 3, 2, 1), (0, 1, 3, 2), (0, 1, 2, 3))
PIECES = 4
ROWS = TOK // PIECES
CCW = ((2, 4, 2, 0), (2, 3, 2, 1), (2, 2, 2, 1), (2, 2, 2, 1))
BLOCKS = BACK + 1
KEYS = BLOCKS * TOK


def kernel(
    n_ctx,
    q_ref,
    k_ref,
    v_ref,
    doc_ref,
    w_ref,
    out_ref,
    kv,
    docs,
    dq,
    m_buf,
    l_buf,
    n_buf,
    a_buf,
    w_buf,
    p_out,
    y_in,
    z_out,
    za_in,
    zd_in,
    q_buf,
    doc_buf,
    own,
    relay,
    loc_sem,
    w_sem,
    wx_send,
    wx_recv,
    kv_send,
    kv_recv,
    doc_send,
    doc_recv,
    fwd_send,
    fwd_recv,
    a_send,
    a_recv,
    y_send,
    y_recv,
    za_send,
    za_recv,
    zd_send,
    zd_recv,
):
    c = lax.axis_index("context")
    t = lax.axis_index("tensor")
    core = lax.rem(t, 2)
    y = lax.rem(t // 2, 4)
    z = t // 8
    other = 1 - core
    lo, hi, whole = pl.ds(0, HALF), pl.ds(HALF, HALF), pl.ds(0, TOK)

    def dev(dz, dy, same_core=True):
        who = core if same_core else other
        return {"tensor": (lax.rem(z + dz, 4) * 4 + lax.rem(y + dy, 4)) * 2 + who}

    x, z_lo = lax.rem(c, 4), c // 4

    def up(d):
        at = z_lo + d
        hi_part = lax.rem(z + at // 8, 4)
        return {"context": lax.rem(at, 8) * 4 + x, "tensor": (hi_part * 4 + y) * 2 + core}

    def down(d):
        at = z_lo + 8 - d
        hi_part = lax.rem(z + 3 + at // 8, 4)
        return {"context": lax.rem(at, 8) * 4 + x, "tensor": (hi_part * 4 + y) * 2 + core}

    def tell(i):
        d = (1, 2, 4)[i]
        for way, where in ((1, up(d)), (0, down(d))):
            pl.semaphore_signal(
                relay.at[i, way], inc=1, device_id=where, device_id_type=MESH
            )

    def hear(i):
        pl.semaphore_wait(relay.at[i, 0], 1)
        pl.semaphore_wait(relay.at[i, 1], 1)

    prompt = jnp.logical_or(z >= 2, jnp.logical_and(z == 0, z_lo == 0))

    barrier = pltpu.get_barrier_semaphore()

    @pl.when(z_lo == 7)
    def _():
        pl.semaphore_signal(barrier, inc=1, device_id=up(1), device_id_type=MESH)

    @pl.when(z_lo == 0)
    def _():
        pl.semaphore_signal(barrier, inc=1, device_id=down(1), device_id_type=MESH)

    for where in (dev(0, 0, False), dev(0, 1), dev(0, 3)):
        pl.semaphore_signal(barrier, inc=1, device_id=where, device_id_type=MESH)
    for k in range(1, BACK + 1):

        @pl.when(c + k < n_ctx)
        def _():
            pl.semaphore_signal(
                barrier, inc=1, device_id={"context": c + k}, device_id_type=MESH
            )

        @pl.when(c >= k)
        def _():
            pl.semaphore_signal(
                barrier, inc=1, device_id={"context": c - k}, device_id_type=MESH
            )

    head = pl.multiple_of((t // 4) * HD, HD)
    k_copy = pltpu.make_async_copy(
        k_ref.at[:, pl.ds(head, HD)], kv.at[0, pl.ds(0, TOK), :], loc_sem.at[0]
    )
    v_copy = pltpu.make_async_copy(
        v_ref.at[:, pl.ds(head, HD)], kv.at[1, pl.ds(0, TOK), :], loc_sem.at[1]
    )
    q_copy = pltpu.make_async_copy(q_ref, q_buf, loc_sem.at[2])
    doc_copy = pltpu.make_async_copy(doc_ref, doc_buf, loc_sem.at[3])
    doc_copy.start()
    k_copy.start()
    q_copy.start()
    v_copy.start()

    def columns(r, q, who):
        u = ORDER[3][r]
        for zi in range(3):
            u = jnp.where(z == zi, ORDER[zi][r], u)
        j = u * 4 + lax.rem(y + OFFSETS[q], 4)
        return pl.ds(pl.multiple_of((j * 2 + who) * TOK, TOK), TOK)

    def w_local(r, q):
        i = r * 4 + q
        return pltpu.make_async_copy(
            w_ref.at[:, columns(r, q, core)], w_buf.at[i, core], w_sem.at[i]
        )

    def w_cross(r, q):
        i = r * 4 + q
        return pltpu.make_async_remote_copy(
            src_ref=w_ref.at[:, columns(r, q, other)],
            dst_ref=w_buf.at[i, core],
            send_sem=wx_send.at[i],
            recv_sem=wx_recv.at[i],
            device_id=dev(0, 0, False),
            device_id_type=MESH,
        )

    def w_cross_in(r, q):
        i = r * 4 + q
        return pltpu.make_async_remote_copy(
            src_ref=w_ref.at[:, columns(r, q, other)],
            dst_ref=w_buf.at[i, other],
            send_sem=wx_send.at[i],
            recv_sem=wx_recv.at[i],
            device_id=dev(0, 0, False),
            device_id_type=MESH,
        )

    for r in range(4):
        for q in range(4):
            w_local(r, q).start()

    doc_copy.wait()
    row = doc_buf[...]
    docs[0] = jnp.broadcast_to(row, (8, TOK))
    dq[...] = jnp.broadcast_to(row, (TOK, TOK)).T
    for k in range(1, BACK + 1):

        @pl.when(c < k)
        def _():
            kv[:, pl.ds(k * TOK, TOK), :] = jnp.zeros((2, TOK, HD), jnp.bfloat16)
            docs[k] = jnp.full((8, TOK), -1, jnp.int32)

    def absorb(k, half):
        span = pl.ds(k * TOK, TOK)
        keys, values = kv[0, span, :], kv[1, span, :]
        mask = dq[half, :] == docs[k, 0:1, :]
        if k == 0:
            first = 0 if half is lo else HALF
            i = lax.broadcasted_iota(jnp.int32, (HALF, TOK), 0) + first
            j = lax.broadcasted_iota(jnp.int32, (HALF, TOK), 1)
            mask = mask & (j <= i)
        for h in range(2):
            s = lax.dot_general(
                q_buf[half, pl.ds(h * HD, HD)],
                keys,
                (((1,), (1,)), ((), ())),
                preferred_element_type=jnp.float32,
            )
            s = jnp.where(mask, s * SCALE, NEG_BIG)
            top = jnp.broadcast_to(jnp.max(s, axis=-1, keepdims=True), (HALF, HD))
            if k > 0:
                before = m_buf[h, half, :]
                top = jnp.maximum(before, top)
                keep = jnp.exp2(before - top)
            e = jnp.exp2(s - jnp.concatenate([top, top], axis=1))
            total = jnp.broadcast_to(jnp.sum(e, axis=-1, keepdims=True), (HALF, HD))
            numer = jnp.dot(e.astype(jnp.bfloat16), values, preferred_element_type=jnp.float32)
            if k > 0:
                total = total + keep * l_buf[h, half, :]
                numer = numer + keep * n_buf[h, half, :]
            if k == BACK:
                a_buf[core, half, pl.ds(h * HD, HD)] = (numer / total).astype(jnp.bfloat16)
            else:
                m_buf[h, half, :] = top
                l_buf[h, half, :] = total
                n_buf[h, half, :] = numer

    k_copy.wait()
    q_copy.wait()
    v_copy.wait()
    absorb(0, lo)
    absorb(0, hi)
    partners = 3 + jnp.minimum(c, BACK) + jnp.minimum(n_ctx - 1 - c, BACK)
    partners = partners + jnp.where(z_lo == 0, 1, 0) + jnp.where(z_lo == 7, 1, 0)
    pl.semaphore_wait(barrier, partners)
    tell(0)

    def kv_out(k):
        return pltpu.make_async_remote_copy(
            src_ref=kv.at[core, pl.ds(0, TOK), :],
            dst_ref=kv.at[core, pl.ds(k * TOK, TOK), :],
            send_sem=kv_send.at[k - 1],
            recv_sem=kv_recv.at[k - 1],
            device_id={"context": c + k},
            device_id_type=MESH,
        )

    def doc_out(k):
        return pltpu.make_async_remote_copy(
            src_ref=docs.at[0],
            dst_ref=docs.at[k],
            send_sem=doc_send.at[k - 1],
            recv_sem=doc_recv.at[k - 1],
            device_id={"context": c + k},
            device_id_type=MESH,
        )

    def forward(k, who):
        return pltpu.make_async_remote_copy(
            src_ref=kv.at[who, pl.ds(k * TOK, TOK), :],
            dst_ref=kv.at[who, pl.ds(k * TOK, TOK), :],
            send_sem=fwd_send.at[k - 1],
            recv_sem=fwd_recv.at[k - 1],
            device_id=dev(0, 0, False),
            device_id_type=MESH,
        )

    for k in range(1, BACK + 1):

        @pl.when(c + k < n_ctx)
        def _():
            doc_out(k).start()
            kv_out(k).start()

    for q in range(4):
        w_cross(0, q).start()

    for k in range(1, BACK + 1):

        @pl.when(c >= k)
        def _():
            kv_out(k).wait_recv()
            forward(k, core).start()

        if k == 3:

            @pl.when(prompt)
            def _():
                hear(0)
                tell(1)

        if k >= 2:

            @pl.when(c >= k - 1)
            def _():
                forward(k - 1, other).wait_recv()
                doc_out(k - 1).wait_recv()

            absorb(k - 1, lo)
            absorb(k - 1, hi)

    for r in range(1, 4):
        for q in range(4):
            w_cross(r, q).start()

    @pl.when(prompt)
    def _():
        hear(1)
        tell(2)

    @pl.when(c >= BACK)
    def _():
        forward(BACK, other).wait_recv()
        doc_out(BACK).wait_recv()

    def a_copy(who, half):
        n = 0 if half is lo else 1
        return pltpu.make_async_remote_copy(
            src_ref=a_buf.at[who, half, :],
            dst_ref=a_buf.at[who, half, :],
            send_sem=a_send.at[n],
            recv_sem=a_recv.at[n],
            device_id=dev(0, 0, False),
            device_id_type=MESH,
        )

    for half in (lo, hi):
        absorb(BACK, half)
        a_copy(core, half).start()

    def w_ready(r, q):
        w_local(r, q).wait()
        w_cross_in(r, q).wait_recv()

    def project(r, q, rows):
        i = r * 4 + q
        p = jnp.dot(a_buf[0, rows, :], w_buf[i, 0], preferred_element_type=jnp.float32)
        p = p + jnp.dot(a_buf[1, rows, :], w_buf[i, 1], preferred_element_type=jnp.float32)
        p_out[r, q, rows, :] = p.astype(jnp.bfloat16)

    def y_copy(r, slot, src):
        return pltpu.make_async_remote_copy(
            src_ref=src,
            dst_ref=y_in.at[r, slot],
            send_sem=y_send.at[r, slot],
            recv_sem=y_recv.at[r, slot],
            device_id=dev(0, 1 if slot % 2 == 0 else 3),
            device_id_type=MESH,
        )

    def y_src(r, slot):
        q, half = ((0, lo), (0, hi), (1, hi), (2, lo), (1, lo), (2, hi))[slot]
        return p_out.at[r, q, half, :]

    def y_start(r, slot):
        y_copy(r, slot, y_src(r, slot)).start()

    def y_got(r, slot):
        y_copy(r, slot, y_src(r, slot)).wait_recv()
        return y_in[r, slot].astype(jnp.float32)

    def first_stage():
        for q in range(4):
            w_ready(0, q)
        for half, (slot_a, slot_d, q_d, q_b) in ((lo, (0, 3, 2, 1)), (hi, (1, 2, 1, 2))):
            a_copy(other, half).wait_recv()
            project(0, 0, half)
            y_start(0, slot_a)
            project(0, q_d, half)
            y_start(0, slot_d)
            project(0, q_b, half)
        project(0, 3, whole)

    def stage(r):
        for q in range(4):
            w_ready(r, q)
        project(r, 0, whole)
        y_start(r, 0)
        y_start(r, 1)
        project(r, 1, whole)
        y_start(r, 2)
        project(r, 2, whole)
        y_start(r, 3)
        project(r, 3, whole)

    def stage_b(r):
        up = p_out[r, 1, lo, :].astype(jnp.float32) + y_got(r, 0)
        p_out[r, 1, lo, :] = up.astype(jnp.bfloat16)
        y_start(r, 4)
        down = p_out[r, 2, hi, :].astype(jnp.float32) + y_got(r, 1)
        p_out[r, 2, hi, :] = down.astype(jnp.bfloat16)
        y_start(r, 5)

    def y_sum(r, half):
        slots = (3, 4) if half is lo else (2, 5)
        return p_out[r, 3, half, :].astype(jnp.float32) + y_got(r, slots[0]) + y_got(r, slots[1])

    def piece(p):
        return pl.ds(p * ROWS, ROWS)

    def cw(part, u):
        return range(PIECES - CCW[part][u])

    def ccw(part, u):
        return range(PIECES - CCW[part][u], PIECES)

    def each_place(act):
        for zi in range(4):
            for part in range(len(CCW)):

                @pl.when(jnp.logical_and(z == zi, z_lo // 2 == part))
                def _():
                    act(zi, part)

    def za_copy(r, way, p):
        return pltpu.make_async_remote_copy(
            src_ref=z_out.at[r, piece(p), :],
            dst_ref=za_in.at[way, p],
            send_sem=za_send.at[way, p],
            recv_sem=za_recv.at[way, p],
            device_id=dev(1 if way == 0 else 3, 0),
            device_id_type=MESH,
        )

    def zd_copy(r, way, p):
        return pltpu.make_async_remote_copy(
            src_ref=z_out.at[r, piece(p), :],
            dst_ref=zd_in.at[way, p],
            send_sem=zd_send.at[way, p],
            recv_sem=zd_recv.at[way, p],
            device_id=dev(1 if way == 0 else 3, 0),
            device_id_type=MESH,
        )

    def step_of(zi, u):
        return ORDER[zi].index(u % 4)

    def direct(zi, part, r, pieces):
        u = ORDER[zi][r]
        role = (u - zi) % 4
        for p in pieces:
            if role == 2 and p in cw(part, u):
                za_copy(r, 0, p).start()
            elif role == 2:
                za_copy(r, 1, p).start()
            elif role == 1 and p in ccw(part, u):
                zd_copy(r, 0, p).start()
            elif role == 3 and p in cw(part, u):
                zd_copy(r, 1, p).start()

    def y_done(r):
        for half, pieces in ((lo, (0, 1)), (hi, (2, 3))):
            z_out[r, half, :] = y_sum(r, half).astype(jnp.bfloat16)

            def act(zi, part):
                if (zi, r) != (3, 2):
                    direct(zi, part, r, pieces)

            each_place(act)

    def add_on(zi, way, p):
        r = step_of(zi, zi + 1 if way == 0 else zi - 1)
        za_copy(r, way, p).wait_recv()
        both = z_out[r, piece(p), :].astype(jnp.float32) + za_in[way, p].astype(jnp.float32)
        z_out[r, piece(p), :] = both.astype(jnp.bfloat16)
        zd_copy(r, way, p).start()

    @pl.when(jnp.logical_not(prompt))
    def _():
        hear(0)
        tell(1)
        hear(1)
        tell(2)

    first_stage()
    stage_b(0)
    stage(1)
    hear(2)
    y_done(0)
    stage_b(1)
    stage(2)
    y_done(1)
    stage_b(2)
    stage(3)
    y_done(2)
    stage_b(3)
    own[lo, :] = y_sum(3, lo)
    own[hi, :] = y_sum(3, hi)

    def relay_sums(zi, part):
        onward = [(0, p) for p in cw(part, (zi + 1) % 4)]
        back = [(1, p) for p in ccw(part, (zi + 3) % 4)]
        first, then = (onward, back) if zi == 3 else (back, onward)
        if zi == 2:
            for i in range(PIECES):
                for way, p in first[i : i + 1] + then[i : i + 1]:
                    add_on(zi, way, p)
        else:
            for way, p in first:
                add_on(zi, way, p)
            if zi == 3:
                direct(3, part, 2, range(PIECES))
            for way, p in then:
                add_on(zi, way, p)

    each_place(relay_sums)

    for p in range(PIECES):
        zd_copy(3, 0, p).wait_recv()
        zd_copy(3, 1, p).wait_recv()
        total = own[piece(p), :] + zd_in[0, p].astype(jnp.float32)
        out_ref[piece(p), :] = (total + zd_in[1, p].astype(jnp.float32)).astype(jnp.bfloat16)

    for k in range(1, BACK + 1):

        @pl.when(c + k < n_ctx)
        def _():
            doc_out(k).wait_send()
            kv_out(k).wait_send()

        @pl.when(c >= k)
        def _():
            forward(k, core).wait_send()

    a_copy(core, lo).wait_send()
    a_copy(core, hi).wait_send()
    for r in range(4):
        for q in range(4):
            w_cross(r, q).wait_send()
        for slot in range(6):
            y_copy(r, slot, y_src(r, slot)).wait_send()
    def sent(zi, part):
        for p in cw(part, (zi + 2) % 4):
            za_copy(0, 0, p).wait_send()
        for p in ccw(part, (zi + 2) % 4):
            za_copy(0, 1, p).wait_send()

    each_place(sent)

    for p in range(PIECES):
        zd_copy(0, 0, p).wait_send()
        zd_copy(0, 1, p).wait_send()


def solution(mesh):
    n_ctx = mesh.shape["context"]

    def body(query_rows, key_rows, value_rows, doc_ids, out_weight):
        dma = pltpu.SemaphoreType.DMA
        bf16, f32 = jnp.bfloat16, jnp.float32
        vmem = pl.BlockSpec(memory_space=pltpu.VMEM)
        hbm = pl.BlockSpec(memory_space=pltpu.HBM)

        def run(*refs):
            kernel(n_ctx, *refs)

        return pl.pallas_call(
            run,
            out_shape=jax.ShapeDtypeStruct((TOK, TOK), bf16),
            in_specs=[hbm, hbm, hbm, hbm, hbm],
            out_specs=vmem,
            scratch_shapes=[
                pltpu.VMEM((2, KEYS, HD), bf16),
                pltpu.VMEM((BLOCKS, 8, TOK), jnp.int32),
                pltpu.VMEM((TOK, TOK), jnp.int32),
                pltpu.VMEM((2, TOK, HD), f32),
                pltpu.VMEM((2, TOK, HD), f32),
                pltpu.VMEM((2, TOK, HD), f32),
                pltpu.VMEM((2, TOK, TOK), bf16),
                pltpu.VMEM((16, 2, TOK, TOK), bf16),
                pltpu.VMEM((4, 4, TOK, TOK), bf16),
                pltpu.VMEM((4, 6, HALF, TOK), bf16),
                pltpu.VMEM((4, TOK, TOK), bf16),
                pltpu.VMEM((2, PIECES, ROWS, TOK), bf16),
                pltpu.VMEM((2, PIECES, ROWS, TOK), bf16),
                pltpu.VMEM((TOK, TOK), bf16),
                pltpu.VMEM((1, TOK), jnp.int32),
                pltpu.VMEM((TOK, TOK), f32),
                pltpu.SemaphoreType.REGULAR((3, 2)),
                dma((4,)),
                dma((16,)),
                dma((16,)),
                dma((16,)),
                dma((BACK,)),
                dma((BACK,)),
                dma((BACK,)),
                dma((BACK,)),
                dma((BACK,)),
                dma((BACK,)),
                dma((2,)),
                dma((2,)),
                dma((4, 6)),
                dma((4, 6)),
                dma((2, PIECES)),
                dma((2, PIECES)),
                dma((2, PIECES)),
                dma((2, PIECES)),
            ],
            compiler_params=pltpu.CompilerParams(
                collective_id=0, has_side_effects=True, vmem_limit_bytes=60 * 2**20
            ),
        )(query_rows, key_rows, value_rows, doc_ids.reshape(1, TOK), out_weight)

    placed = (
        P("context", "tensor"),
        P("context", None),
        P("context", None),
        P("context"),
        P("tensor", None),
    )
    return jax.shard_map(
        body, mesh=mesh, in_specs=placed, out_specs=P("context", "tensor"), check_vma=False
    )
```

time: 88.4 us -> 86.8 us (0.982)
  the two profiles are of different devices: /device:TPU:4 before, /device:TPU:264 now
where the time goes in v2:
time: 86.8 us; the launch traced here: 86.6 us
  Pallas kernels  85 us (98%)
  local copies, waits for them, and re-layouts  1.57 us (2%)
    pallas_call x1, Pallas kernels, body(): pl.pallas_call(run, out_shape=jax.ShapeDtypeStruct((TOK, TOK), bf16), in_...  85 us

profile of v2, /device:TPU:264, one launch (start us, length us, event | category | flops | bytes accessed | tf_op | source)
XLA Modules:
  0.0 86.6 jit_solution(2931119204047592992)
XLA Ops:
  0.0 85.0 %shard_map.55 = bf16[256,256]{1,0:T(8,128)(2,1)} custom-call(bf16[256,256]{1,0:T(8,128)(2,1)} %refs_0_.1, bf16[256,1024]{1,0:T(8,128)(2,1)} %refs_1_.1, bf16[256,1024]{1,0:T(8,128)(2,1)} %refs_2_.1, s32[1,256]{1,0:T(1,128)} %bitcast.1, bf16[256,8192]{1,0:T(8,128)(2,1)} %refs_4_.1), custom_call_target="tpu_custom_call" | custom-call | tf_op jit(solution)/shard_map/pallas_call | solution.py:560
  85.0 1.6 %copy.7 = bf16[256,256]{1,0:T(8,128)(2,1)} copy(bf16[256,256]{1,0:T(8,128)(2,1)} %shard_map.55) | data formatting | bytes 262144

commit v3 on v2

--- a/solution.py
+++ b/solution.py
@@ -14,10 +14,10 @@
 SCALE = HD**-0.5 * 1.4426950408889634
 MESH = pl.DeviceIdType.MESH
 OFFSETS = (2, 1, 3, 0)
-ORDER = ((1, 2, 3, 0), (0, 3, 2, 1), (0, 1, 3, 2), (0, 1, 2, 3))
+ORDER = ((1, 2, 3, 0), (0, 3, 2, 1), (0, 1, 3, 2), (1, 0, 2, 3))
 PIECES = 4
 ROWS = TOK // PIECES
-CCW = ((2, 4, 2, 0), (2, 3, 2, 1), (2, 2, 2, 1), (2, 2, 2, 1))
+CCW = ((2, 3, 2, 1), (2, 2, 2, 1), (2, 2, 2, 2), (2, 2, 2, 2))
 BLOCKS = BACK + 1
 KEYS = BLOCKS * TOK
 
@@ -90,22 +90,25 @@
         hi_part = lax.rem(z + 3 + at // 8, 4)
         return {"context": lax.rem(at, 8) * 4 + x, "tensor": (hi_part * 4 + y) * 2 + core}
 
+    def tell_one(i, way):
+        d = (1, 2, 4)[i]
+        where = up(d) if way == 1 else down(d)
+        pl.semaphore_signal(relay.at[i, way], inc=1, device_id=where, device_id_type=MESH)
+
     def tell(i):
-        d = (1, 2, 4)[i]
-        for way, where in ((1, up(d)), (0, down(d))):
-            pl.semaphore_signal(
-                relay.at[i, way], inc=1, device_id=where, device_id_type=MESH
-            )
+        tell_one(i, 1)
+        tell_one(i, 0)
 
     def hear(i):
         pl.semaphore_wait(relay.at[i, 0], 1)
         pl.semaphore_wait(relay.at[i, 1], 1)
 
-    prompt = jnp.logical_or(z >= 2, jnp.logical_and(z == 0, z_lo == 0))
+    prompt = z >= 2
+    first_plane = jnp.logical_and(z == 0, z_lo == 0)
 
     barrier = pltpu.get_barrier_semaphore()
 
-    @pl.when(z_lo == 7)
+    @pl.when(jnp.logical_and(z_lo == 7, z < 3))
     def _():
         pl.semaphore_signal(barrier, inc=1, device_id=up(1), device_id_type=MESH)
 
@@ -234,9 +237,13 @@
     absorb(0, lo)
     absorb(0, hi)
     partners = 3 + jnp.minimum(c, BACK) + jnp.minimum(n_ctx - 1 - c, BACK)
-    partners = partners + jnp.where(z_lo == 0, 1, 0) + jnp.where(z_lo == 7, 1, 0)
+    partners = partners + jnp.where(jnp.logical_and(z_lo == 0, z > 0), 1, 0)
+    partners = partners + jnp.where(z_lo == 7, 1, 0)
     pl.semaphore_wait(barrier, partners)
-    tell(0)
+
+    @pl.when(jnp.logical_not(first_plane))
+    def _():
+        tell(0)
 
     def kv_out(k):
         return pltpu.make_async_remote_copy(
@@ -452,7 +459,7 @@
                 zd_copy(r, 1, p).start()
 
     def y_done(r):
-        for half, pieces in ((lo, (0, 1)), (hi, (2, 3))):
+        for half, pieces in ((lo, range(PIECES // 2)), (hi, range(PIECES // 2, PIECES))):
             z_out[r, half, :] = y_sum(r, half).astype(jnp.bfloat16)
 
             def act(zi, part):
@@ -471,6 +478,11 @@
     @pl.when(jnp.logical_not(prompt))
     def _():
         hear(0)
+
+        @pl.when(first_plane)
+        def _():
+            tell(0)
+
         tell(1)
         hear(1)
         tell(2)

time: 86.8 us -> 81.3 us (0.937)
  the two profiles are of different devices: /device:TPU:264 before, /device:TPU:4 now
where the time goes in v3:
time: 81.3 us; the launch traced here: 81.1 us
  Pallas kernels  79.5 us (98%)
  local copies, waits for them, and re-layouts  1.57 us (2%)
    pallas_call x1, Pallas kernels, body(): pl.pallas_call(run, out_shape=jax.ShapeDtypeStruct((TOK, TOK), bf16), in_...  79.5 us

profile of v3, /device:TPU:4, one launch (start us, length us, event | category | flops | bytes accessed | tf_op | source)
XLA Modules:
  0.0 81.1 jit_solution(4362890943839080602)
XLA Ops:
  0.0 79.5 %shard_map.55 = bf16[256,256]{1,0:T(8,128)(2,1)} custom-call(bf16[256,256]{1,0:T(8,128)(2,1)} %refs_0_.1, bf16[256,1024]{1,0:T(8,128)(2,1)} %refs_1_.1, bf16[256,1024]{1,0:T(8,128)(2,1)} %refs_2_.1, s32[1,256]{1,0:T(1,128)} %bitcast.1, bf16[256,8192]{1,0:T(8,128)(2,1)} %refs_4_.1), custom_call_target="tpu_custom_call" | custom-call | tf_op jit(solution)/shard_map/pallas_call | solution.py:572
  79.5 1.6 %copy.7 = bf16[256,256]{1,0:T(8,128)(2,1)} copy(bf16[256,256]{1,0:T(8,128)(2,1)} %shard_map.55) | data formatting | bytes 262144

commit v4 on v3

--- a/solution.py
+++ b/solution.py
@@ -612,7 +612,7 @@
                 dma((2, PIECES)),
             ],
             compiler_params=pltpu.CompilerParams(
-                collective_id=0, has_side_effects=True, vmem_limit_bytes=60 * 2**20
+                collective_id=0, has_side_effects=True, vmem_limit_bytes=52 * 2**20
             ),
         )(query_rows, key_rows, value_rows, doc_ids.reshape(1, TOK), out_weight)
 

time: 81.3 us -> 80.9 us (level)
  the two profiles are of different devices: /device:TPU:4 before, /device:TPU:128 now
where the time goes in v4:
time: 80.9 us; the launch traced here: 80.7 us
  Pallas kernels  76.3 us (94%)
  local copies, waits for them, and re-layouts  4.32 us (5%)
    pallas_call x1, Pallas kernels, body(): pl.pallas_call(run, out_shape=jax.ShapeDtypeStruct((TOK, TOK), bf16), in_...  76.3 us
    unnamed x9, local copies, waits for them, and re-layouts  4.32 us

profile of v4, /device:TPU:128, one launch (start us, length us, event | category | flops | bytes accessed | tf_op | source)
XLA Modules:
  0.0 80.7 jit_solution(4507590764612704401)
XLA Ops:
  0.0 0.0 copy-start
  0.0 1.0 %copy-done = bf16[256,1024]{1,0:T(8,128)(2,1)S(1)} copy-done((bf16[256,1024]{1,0:T(8,128)(2,1)S(1)}, bf16[256,1024]{1,0:T(8,128)(2,1)}, u32[]{:S(2)}) %copy-start) | copy-done | bytes 524312
  1.0 0.0 copy-start.1
  1.0 1.0 %copy-done.1 = bf16[256,1024]{1,0:T(8,128)(2,1)S(1)} copy-done((bf16[256,1024]{1,0:T(8,128)(2,1)S(1)}, bf16[256,1024]{1,0:T(8,128)(2,1)}, u32[]{:S(2)}) %copy-start.1) | copy-done | bytes 524312
  2.1 0.0 copy-start.2
  2.1 0.9 %copy-done.2 = bf16[256,256]{1,0:T(8,128)(2,1)S(1)} copy-done((bf16[256,256]{1,0:T(8,128)(2,1)S(1)}, bf16[256,256]{1,0:T(8,128)(2,1)}, u32[]{:S(2)}) %copy-start.2) | copy-done | bytes 131096
  3.0 0.0 copy-start.3
  3.0 0.7 copy-done.3
  3.7 76.3 %shard_map.55 = bf16[256,256]{1,0:T(8,128)(2,1)S(1)} custom-call(bf16[256,256]{1,0:T(8,128)(2,1)S(1)} %copy-done.2, bf16[256,1024]{1,0:T(8,128)(2,1)S(1)} %copy-done, bf16[256,1024]{1,0:T(8,128)(2,1)S(1)} %copy-done.1, s32[1,256]{1,0:T(1,128)S(1)} %bitcast.1, bf16[256,8192]{1,0:T(8,128)(2,1)} %refs_4_.1), custom_call_target="tpu_custom_call" | custom-call | tf_op jit(solution)/shard_map/pallas_call | solution.py:572
  80.0 0.7 copy.7
Async XLA Ops:
  0.0 1.0 %copy-start = (bf16[256,1024]{1,0:T(8,128)(2,1)S(1)}, bf16[256,1024]{1,0:T(8,128)(2,1)}, u32[]{:S(2)}) copy-start(bf16[256,1024]{1,0:T(8,128)(2,1)} %refs_1_.1) | copy-start | bytes 1572868
  1.0 1.0 %copy-start.1 = (bf16[256,1024]{1,0:T(8,128)(2,1)S(1)}, bf16[256,1024]{1,0:T(8,128)(2,1)}, u32[]{:S(2)}) copy-start(bf16[256,1024]{1,0:T(8,128)(2,1)} %refs_2_.1) | copy-start | bytes 1572868
  2.1 0.9 %copy-start.2 = (bf16[256,256]{1,0:T(8,128)(2,1)S(1)}, bf16[256,256]{1,0:T(8,128)(2,1)}, u32[]{:S(2)}) copy-start(bf16[256,256]{1,0:T(8,128)(2,1)} %refs_0_.1) | copy-start | bytes 393220
  3.0 0.7 copy-start.3
